TPU v7x, 128 devices: a whole 4x4x4 slice. The times are simulated.
128 devices in a mesh: dp: 8 (over x, z_lo), tensor: 16 (over y, z_hi, core).
Axes of the slice: x: 4, y: 4, z: 4 (z_hi: 2, z_lo: 2; z = z_hi * 2 + z_lo), core: 2. Of those that a mesh axis runs over, the one named last changes fastest.
Arguments:
- hidden_act: bfloat16 [5632, 36864], P('dp', 'tensor'), may hold values from -80 to 80
- out_grad: bfloat16 [5632, 4608], P('dp', 'tensor'), may hold values from -0.5 to 0.5
- other_sq: float32 [16], P('dp'), may hold values from 2989699 to 597939968
Outputs:
- weight_grad: float32 [4608, 36864], P('dp', 'tensor')
All inputs are finite; a program needn't handle non-finite values.
Results may differ from a plain program's by a relative error of at most 0.002.
Values may be sent and summed in bfloat16 or wider, within the bound.
A program may use at most 128 MiB of HBM per device.

v0:
```python
import math

import jax
import jax.numpy as jnp
from jax import lax
from jax.sharding import Mesh
from jax.sharding import PartitionSpec as P

D = 4608
FF = 36864
L = 352
DP = ("dp_0", "dp_1")


def in_blocks(array, dim, length):
    dims = array.shape
    blocks = array.reshape(*dims[:dim], length, dims[dim] // length, *dims[dim + 1 :])
    return jnp.moveaxis(blocks, dim, 0)


def sum_at_owner(array, axis, dim):
    length = lax.axis_size(axis)
    blocks = lax.all_to_all(in_blocks(array, dim, length), axis, 0, 0, tiled=True)
    return jnp.sum(blocks, axis=0)


def sent_to_all(array, axis):
    length = lax.axis_size(axis)
    return lax.all_to_all(
        jnp.broadcast_to(array[None], (length, *array.shape)), axis, 0, 0, tiled=True
    )


def over_copies(array, axis):
    everything = sent_to_all(array, axis)
    return jnp.sum(everything, axis=0)


def summed_rows(subtotal, axes):
    for axis in axes:
        subtotal = lax.psum_scatter(subtotal, axis, scatter_dimension=0, tiled=True)
    return subtotal


def on_device(hidden_act, out_grad, other_sq):
    examples_here = other_sq.shape[0]
    length = hidden_act.shape[0] // examples_here
    hidden_blocks = hidden_act.reshape(examples_here, length, hidden_act.shape[1])
    act_gram = jnp.einsum(
        "etf,esf->ets", hidden_blocks, hidden_blocks, preferred_element_type=jnp.float32
    )
    full_grad = lax.all_gather(out_grad, "tensor", axis=1, tiled=True)
    grad_blocks = full_grad.reshape(examples_here, length, full_grad.shape[1])
    act_share = sum_at_owner(act_gram, "tensor", 1)
    share_rows = act_share.shape[1]
    row_start = lax.axis_index("tensor") * share_rows
    grad_share = lax.dynamic_slice_in_dim(grad_blocks, row_start, share_rows, 1)
    grad_gram_rows = jnp.einsum(
        "etd,esd->ets", grad_share, grad_blocks, preferred_element_type=jnp.float32
    )
    layer_sq = over_copies(jnp.sum(act_share * grad_gram_rows, axis=(1, 2)), "tensor")
    clip_bound = math.sqrt(L * FF * D / 80.0)
    clip_scale = jnp.minimum(1.0, clip_bound / jnp.sqrt(other_sq + layer_sq))
    scaled_grad = (grad_blocks.astype(jnp.float32) * clip_scale[:, None, None]).astype(jnp.bfloat16)
    scaled_grad = scaled_grad.reshape(examples_here * length, full_grad.shape[1])
    contract_rows = (((0,), (0,)), ((), ()))
    return summed_rows(
        lax.dot_general(scaled_grad, hidden_act, contract_rows, preferred_element_type=jnp.float32),
        DP,
    )


def solution(mesh):
    torus = Mesh(mesh.devices.reshape(4, 2, mesh.shape["tensor"]), ("dp_0", "dp_1", "tensor"))
    in_specs = (P(DP, "tensor"), P(DP, "tensor"), P(DP))
    out_specs = P(DP, "tensor")
    return jax.shard_map(
        on_device, mesh=torus, in_specs=in_specs, out_specs=out_specs, check_vma=False
    )
```

profile of v0, /device:TPU:0, one launch (start us, length us, event | category | flops | bytes accessed | tf_op | source)
XLA Modules:
  0.0 624.7 jit_solution(8400824350638153253)
XLA Ops:
  6.5 0.0 copy-start
  6.5 0.0 all-gather.2.cloned.1.call-start
  6.5 0.7 all-gather.2.cloned.1.call-update
  7.3 1.2 copy-done
  8.5 1.8 fusion.5
  10.3 1.8 copy.13
  12.1 8.0 %all-to-all-start = ((f32[16,2,22,352]{3,1,2,0:T(2,128)}), f32[16,2,22,352]{3,1,2,0:T(2,128)}, u32[]{:S(2)}, u32[]{:S(2)}) async-start(f32[16,2,22,352]{3,1,2,0:T(2,128)} %bitcast.11), calls=%async_computation | async-start | bytes 2162688 | tf_op jit(solution)/shard_map/all_to_all | solution.py:23
  20.2 0.0 reduce-scatter.3.cloned.1.call-start
  20.2 22.3 %all-to-all-done = f32[16,2,22,352]{3,1,2,0:T(2,128)} async-done(((f32[16,2,22,352]{3,1,2,0:T(2,128)}), f32[16,2,22,352]{3,1,2,0:T(2,128)}, u32[]{:S(2)}, u32[]{:S(2)}) %all-to-all-start) | async-done | bytes 991264 | tf_op jit(solution)/shard_map/all_to_all | solution.py:23
  42.5 1.6 reduce_sum.27
  44.1 43.1 %all-gather.2.cloned.1.call-done = bf16[704,4608]{0,1:T(8,128)(2,1)} async-done(((bf16[704,288]{0,1:T(8,128)(2,1)}), bf16[704,4608]{0,1:T(8,128)(2,1)}) %all-gather.2.cloned.1.call-update) | async-done | bytes 6488080 | tf_op jit(solution)/shard_map/all_gather | solution.py:52
  87.3 9.4 %copy.14 = bf16[704,4608]{1,0:T(8,128)(2,1)} copy(bf16[704,4608]{0,1:T(8,128)(2,1)} %all-gather.2.cloned.1.call-done) | data formatting | bytes 12976128 | tf_op jit(solution)/shard_map/all_gather | solution.py:52
  96.7 0.0 copy-start.2
  96.7 4.9 fusion.2
  101.7 10.5 %all_to_all.11 = f32[16,1,2]{2,1,0:T(1,128)S(1)} all-to-all(f32[16,1,2]{2,1,0:T(1,128)S(1)} %broadcast_in_dim.2), channel_id=1, replica_groups=mesh['dp_0'=4,'dp_1'=2,'tensor'=16] {'tensor'}, dimensions={0} | all-to-all | bytes 256 | tf_op jit(solution)/shard_map/all_to_all | solution.py:29
  112.2 0.0 copy-done.2
  112.3 0.1 mul.21
  112.3 0.1 mul.22
  112.4 25.2 %fusion = f32[4608,2304]{1,0:T(8,128)} fusion(bf16[704,2304]{1,0:T(8,128)(2,1)S(1)} %copy-done, bf16[704,4608]{0,1:T(8,128)(2,1)} %all-gather.2.cloned.1.call-done, f32[704]{0:T(1024)S(1)} %mul.22), kind=kOutput, calls=%fused_computation.1 | convolution fusion | flops 14958231552 | bytes 52202240 | tf_op jit(solution)/shard_map/dot_general | solution.py:68
  137.6 0.0 reduce-scatter.3.cloned.1.call-update
  137.7 0.0 copy-start.1
  137.7 0.0 reduce-scatter.5.cloned.1.call-start
  137.7 352.3 %reduce-scatter.3.cloned.1.call-done = f32[1152,2304]{1,0:T(8,128)} async-done(((f32[4608,2304]{1,0:T(8,128)}), f32[1152,2304]{1,0:T(8,128)}) %reduce-scatter.3.cloned.1.call-update) | async-done | bytes 10616848 | tf_op jit(solution)/shard_map/reduce_scatter | solution.py:41
  490.0 0.0 reduce-scatter.5.cloned.1.call-update
  490.0 128.1 %reduce-scatter.5.cloned.1.call-done = f32[576,2304]{1,0:T(8,128)} async-done(((f32[1152,2304]{1,0:T(8,128)}), f32[576,2304]{1,0:T(8,128)}) %reduce-scatter.5.cloned.1.call-update) | async-done | bytes 5308432 | tf_op jit(solution)/shard_map/reduce_scatter | solution.py:41
  618.1 0.0 copy-done.1
  (3 shorter events, 0.1 us)
Async XLA Ops:
  6.5 1.9 copy-start
  6.5 80.7 %all-gather.2.cloned.1.call-start = ((), (), s32[]{:S(2)}) async-start(), calls=%async_computation.4 | async-start | bytes 7520256 | tf_op jit(solution)/shard_map/all_gather | solution.py:52
  12.1 30.4 %all-to-all-start = ((f32[16,2,22,352]{3,1,2,0:T(2,128)}), f32[16,2,22,352]{3,1,2,0:T(2,128)}, u32[]{:S(2)}, u32[]{:S(2)}) async-start(f32[16,2,22,352]{3,1,2,0:T(2,128)} %bitcast.11), calls=%async_computation | async-start | bytes 2162688 | tf_op jit(solution)/shard_map/all_to_all | solution.py:23
  20.2 469.8 %reduce-scatter.3.cloned.1.call-start = ((), (), s32[]{:S(2)}) async-start(), calls=%async_computation.5 | async-start | bytes 53084160 | tf_op jit(solution)/shard_map/reduce_scatter | solution.py:41
  96.7 15.5 %copy-start.2 = (f32[2]{0:T(128)S(1)}, f32[2]{0:T(128)}, u32[]{:S(2)}) copy-start(f32[2]{0:T(128)} %param.5) | copy-start | bytes 28
  137.7 480.5 %copy-start.1 = (bf16[704,2304]{1,0:T(8,128)(2,1)S(1)}, bf16[704,2304]{1,0:T(8,128)(2,1)}, u32[]{:S(2)}) copy-start(bf16[704,2304]{1,0:T(8,128)(2,1)} %param.3) | copy-start | bytes 9732100
  137.7 480.5 %reduce-scatter.5.cloned.1.call-start = ((), (), s32[]{:S(2)}) async-start(), calls=%async_computation.6 | async-start | bytes 15925248 | tf_op jit(solution)/shard_map/reduce_scatter | solution.py:41
Sparse Core Ops, SparseCore 0:
  9.7 77.5 all-gather.1
  137.8 352.1 reduce-scatter.2
  492.4 125.6 reduce-scatter.4
where the time goes:
time: 626 us; the launch traced here: 625 us
  waiting for transfers between devices  547 us (87%)
  matrix products  32 us (5%)
  between operations  13.2 us (2%)
  local copies, waits for them, and re-layouts  12.6 us (2%)
  blocking collectives  10.5 us (2%)
  starting transfers between devices  8.13 us (1%)
    reduce_scatter x2, waiting for transfers between devices, summed_rows(): subtotal = lax.psum_scatter(subtotal, axis, scatter_dimension=0, tiled=True)  480 us
    all_gather x1, waiting for transfers between devices, on_device(): full_grad = lax.all_gather(out_grad, 'tensor', axis=1, tiled=True)  43.1 us
    dot_general x1, matrix products, on_device(): lax.dot_general(scaled_grad, hidden_act, contract_rows, preferred_element...  25.2 us
    all_to_all x1, waiting for transfers between devices, sum_at_owner(): lax.all_to_all(in_blocks(array, dim, length), axis, 0, 0, tiled=True)  22.3 us
  transfers between devices with their start and end apart: 4, of which 4 were waited for; matrix products, arithmetic and copies ran while one was open for 1% of the time, Pallas kernels for 0%

commit v1 on v0

v1 whole, which is shorter than its diff:
```python
import functools
import math

import jax
import jax.numpy as jnp
from jax import lax
from jax.experimental import pallas as pl
from jax.experimental.pallas import tpu as pltpu
from jax.sharding import Mesh
from jax.sharding import PartitionSpec as P

D = 4608
FF = 36864
L = 352
TOK = 2 * L
COLS = 2304
HALF = COLS // 2
FEAT = 288
W = 128
NC = HALF // W
AXES = ("x", "zl", "y", "zh", "c")
MESH = pl.DeviceIdType.MESH
BOUND = math.sqrt(L * FF * D / 80.0)
NT = (((1,), (1,)), ((), ()))
ROWS = L // 4


def kernel(
    hid_hbm, gt_hbm, g_hbm, other_ref, out_hbm,
    hid, bb, at, gv, gh, rc, rd, ry, r2, rz, tl, ty, tc, tz, tx, sv, cs, co,
    ld_s, lb_s, t_s, sw_s, sw_r, x_s, x_r, az_s, az_r, ay_s, ay_r, ac_s, ac_r,
    g1_s, g2_s, g2_r, g3_s, t1_s, t1_r, t2_s, t4_s, t4_r, c_s, c_r, o_s,
):
    x, zl, y, zh, c = (lax.axis_index(a) for a in AXES)
    z = zh * 2 + zl
    xr, xl, xo = (x + 1) % 4, (x + 3) % 4, (x + 2) % 4
    yr, yl, yo = (y + 1) % 4, (y + 3) % 4, (y + 2) % 4

    def dev(nx=None, nz=None, ny=None, nc=None):
        nz = z if nz is None else nz
        return (
            x if nx is None else nx,
            nz % 2,
            y if ny is None else ny,
            nz // 2,
            c if nc is None else nc,
        )

    zpair = zh * 2 + (1 - zl)

    def send(src, dst, ss, rs, to):
        return pltpu.make_async_remote_copy(
            src_ref=src, dst_ref=dst, send_sem=ss, recv_sem=rs,
            device_id=to, device_id_type=MESH,
        )

    keep = zl * HALF
    give = (1 - zl) * HALF

    load_hid = pltpu.make_async_copy(hid_hbm, hid, ld_s.at[0])
    load_g = pltpu.make_async_copy(g_hbm, gv, ld_s.at[1])
    load_hid.start()

    def load_own(k):
        col = pl.multiple_of(keep + k * W, W)
        return pltpu.make_async_copy(
            hid_hbm.at[:, pl.ds(col, W)], bb.at[k, x, zl], lb_s.at[k]
        )

    load_g.start()

    @pl.loop(0, NC)
    def _(k):
        load_own(k).start()

    load_t = pltpu.make_async_copy(gt_hbm, at.at[y, z, c], ld_s.at[2])

    @pl.when(x == y)
    def _():
        load_t.start()

    bar = pltpu.get_barrier_semaphore()
    partners = [dev(nx=v) for v in (xr, xl, xo)]
    partners += [dev(ny=v) for v in (yr, yl, yo)]
    partners += [dev(nz=(z + d) % 4) for d in (1, 2, 3)]
    partners += [dev(nc=1 - c)]
    for to in partners:
        pl.semaphore_signal(bar, inc=1, device_id=to, device_id_type=MESH)

    @pl.when(x != y)
    def _():
        pl.semaphore_signal(bar, inc=1, device_id=dev(nx=y, ny=x), device_id_type=MESH)

    pl.semaphore_wait(bar, len(partners) + (x != y).astype(jnp.int32))

    def t_copy():
        return send(gt_hbm, at.at[x, z, c], t_s.at[0], t_s.at[1], dev(nx=y, ny=x))

    @pl.when(x != y)
    def _():
        t_copy().start()

    load_hid.wait()

    def swap(k):
        col = pl.multiple_of(give + k * W, W)
        return send(
            hid.at[:, pl.ds(col, W)], bb.at[k, x, zl], sw_s.at[k], sw_r.at[k],
            dev(nz=zpair),
        )

    for k in range(3):
        swap(k).start()

    def x_copies(k):
        return (
            send(bb.at[k, x], bb.at[k, x], x_s.at[0, k], x_r.at[0, k], dev(nx=xr)),
            send(bb.at[k, x], bb.at[k, x], x_s.at[1, k], x_r.at[1, k], dev(nx=xl)),
        )

    def f_copies(k):
        return (
            send(bb.at[k, xl, 0], bb.at[k, xl, 0], x_s.at[2, k], x_r.at[2, k], dev(nx=xr)),
            send(bb.at[k, xr, 1], bb.at[k, xr, 1], x_s.at[3, k], x_r.at[3, k], dev(nx=xl)),
        )

    def send_x(k):
        load_own(k).wait()
        swap(k).wait_recv()
        for copy in x_copies(k):
            copy.start()

    def fwd_x(k):
        for near, copy in zip(x_copies(k), f_copies(k)):
            near.wait_recv()
            copy.start()

    def far_x(k):
        for copy in f_copies(k):
            copy.wait_recv()

    @pl.loop(0, 2)
    def _(e):
        rows = pl.ds(pl.multiple_of(e * L, 32), L)
        h = hid[rows, :]
        gh[e, 0] = lax.dot_general(h, h, NT, preferred_element_type=jnp.float32)

    load_g.wait()

    @pl.loop(0, 2)
    def _(e):
        rows = pl.ds(pl.multiple_of(e * L, 32), L)
        g = gv[rows, :]
        gh[e, 1] = lax.dot_general(g, g, NT, preferred_element_type=jnp.float32)

    g1 = send(gh.at[1 - c], rc, g1_s.at[0], g1_s.at[1], dev(nc=1 - c))
    g1.start()

    send_x(0)
    swap(3).start()

    @pl.when(x != y)
    def _():
        t_copy().wait()

    @pl.when(x == y)
    def _():
        load_t.wait()

    def z_copy(d):
        return send(
            at.at[y, z, c], at.at[y, z, c], az_s.at[d - 1], az_r.at[d - 1],
            dev(nz=(z + d) % 4),
        )

    for d in (1, 3, 2):
        z_copy(d).start()

    g1.wait()
    rd[...] = gh[c] + rc[...]

    def g2(d):
        to = (y + d) % 4
        rows = pl.ds(pl.multiple_of(to * ROWS, 8), ROWS)
        return send(
            rd.at[:, rows, :], ry.at[d - 1], g2_s.at[d - 1], g2_r.at[d - 1], dev(ny=to)
        )

    for d in (1, 3, 2):
        g2(d).start()

    send_x(1)
    swap(4).start()

    def block(q):
        high = 1 - zl if q < 2 else zl
        low = zl if q % 2 == 0 else 1 - zl
        return high * 2 + low

    top, bottom = pl.ds(0, FEAT // 2), pl.ds(FEAT // 2, FEAT // 2)

    def y_copies(q):
        b = at.at[y, block(q), c]
        return (
            send(b, b, ay_s.at[0, q], ay_r.at[0, q], dev(ny=yr)),
            send(b, b, ay_s.at[1, q], ay_r.at[1, q], dev(ny=yl)),
        )

    def yf_copies(q):
        a = at.at[yl, block(q), c, top]
        b = at.at[yr, block(q), c, bottom]
        return (
            send(a, a, ay_s.at[2, q], ay_r.at[2, q], dev(ny=yr)),
            send(b, b, ay_s.at[3, q], ay_r.at[3, q], dev(ny=yl)),
        )

    def core_copy(q, j):
        b = at.at[(y, yl, yr, yo)[j], block(q), c]
        return send(b, b, ac_s.at[j, q], ac_r.at[j, q], dev(nc=1 - c))

    def own_y(q):
        d = (z - block(q) + 4) % 4

        @pl.when(d != 0)
        def _():
            i = jnp.maximum(d - 1, 0)
            send(
                at.at[y, block(q), c], at.at[y, block(q), c], az_s.at[i], az_r.at[i],
                dev(nz=zpair),
            ).wait_recv()

        for copy in y_copies(q):
            copy.start()
        core_copy(q, 0).start()

    def fwd_y(q):
        for j, (near, copy) in enumerate(zip(y_copies(q), yf_copies(q))):
            near.wait_recv()
            copy.start()
            core_copy(q, 1 + j).start()

    def far_y(q):
        for copy in yf_copies(q):
            copy.wait_recv()
        core_copy(q, 3).start()

    def settle(q):
        for copy in y_copies(q) + yf_copies(q):
            copy.wait_send()
        for j in range(4):
            core_copy(q, j).wait()

    own_y(0)

    for d in (1, 3, 2):
        g2(d).wait()
    mine = pl.ds(pl.multiple_of(y * ROWS, 8), ROWS)
    r2[...] = rd[:, mine, :] + ry[0] + ry[1] + ry[2]
    g3 = send(r2, rz, g3_s.at[0], g3_s.at[1], dev(nz=(z + 2) % 4))
    g3.start()

    send_x(2)
    swap(5).start()

    g3.wait()
    total = r2[...] + rz[...]
    part = jnp.sum(total[0] * total[1])
    lane = lax.broadcasted_iota(jnp.int32, (8, W), 1)
    example = (x * 2 + zl) * 2 + c
    other = jnp.where(c == 0, other_ref[0], other_ref[1])
    tile = jnp.where(lane == example * 4 + y, part, 0.0)
    tl[0] = tile + jnp.where((lane == 64 + example) & (y == 0), other, 0.0)

    def t1(d):
        return send(
            tl.at[0], ty.at[d - 1], t1_s.at[d - 1], t1_r.at[d - 1], dev(ny=(y + d) % 4)
        )

    for d in (1, 3, 2):
        t1(d).start()

    fwd_x(0)

    for d in (1, 3, 2):
        t1(d).wait()
    tl[1] = tl[0] + ty[0] + ty[1] + ty[2]
    t2 = send(tl.at[1], tc, t2_s.at[0], t2_s.at[1], dev(nc=1 - c))
    t2.start()
    t2.wait()
    tl[2] = tl[1] + tc[...]
    t3 = send(tl.at[2], tz, t2_s.at[2], t2_s.at[3], dev(nz=zpair))
    t3.start()
    t3.wait()
    tl[3] = tl[2] + tz[...]

    def t4(d):
        return send(
            tl.at[3], tx.at[d - 1], t4_s.at[d - 1], t4_r.at[d - 1], dev(nx=(x + d) % 4)
        )

    for d in (1, 3, 2):
        t4(d).start()

    own_y(1)
    send_x(3)
    swap(6).start()
    fwd_y(0)
    fwd_x(1)
    send_x(4)
    swap(7).start()

    for d in (1, 3, 2):
        t4(d).wait()
    full = (tl[3] + tx[0] + tx[1] + tx[2])[0:1]
    row = lax.broadcasted_iota(jnp.int32, (1, W), 1)
    token = lax.broadcasted_iota(jnp.int32, (1, TOK), 1)
    for g in range(8):
        pair = []
        for e in (2 * g, 2 * g + 1):
            layer = jnp.sum(
                jnp.where((row >= 4 * e) & (row < 4 * e + 4), full, 0.0), axis=1, keepdims=True
            )
            rest = jnp.sum(jnp.where(row == 64 + e, full, 0.0), axis=1, keepdims=True)
            pair.append(jnp.minimum(1.0, BOUND / jnp.sqrt(rest + layer)))
        sv[g] = jnp.where(token < L, pair[0], pair[1])

    fwd_y(1)
    far_y(0)
    fwd_x(2)
    own_y(2)
    send_x(5)
    swap(8).start()
    far_y(1)
    fwd_x(3)

    def scale(q):
        settle(q)

        @pl.loop(0, 8)
        def _(i):
            yy, cc = i // 2, i % 2
            s = sv[yy * 2 + block(q) % 2]
            b = at[yy, block(q), cc].astype(jnp.float32)
            at[yy, block(q), cc] = (b * s).astype(jnp.bfloat16)

    def multiply(k, high, dst):
        @pl.loop(0, 2)
        def _(cc):
            acc = None
            for xs in range(4):
                for zs in range(2):
                    p = jnp.dot(
                        at[xs, high * 2 + zs, cc], bb[k, xs, zs],
                        preferred_element_type=jnp.float32,
                    )
                    acc = p if acc is None else acc + p
            dst[k, pl.ds(pl.multiple_of(cc * FEAT, 32), FEAT), :] = acc

    def out_cols(k):
        return out_hbm.at[:, pl.ds(pl.multiple_of(keep + k * W, W), W)]

    def c_copy(k):
        return send(cs.at[k], out_cols(k), c_s.at[k], c_r.at[k], dev(nz=zpair))

    def o_copy(k):
        return pltpu.make_async_copy(co.at[k], out_cols(k), o_s.at[k])

    def give_out(k):
        multiply(k, 1 - zl, cs)
        c_copy(k).start()

    def keep_out(k):
        multiply(k, zl, co)
        o_copy(k).start()

    for d in (1, 3, 2):
        z_copy(d).wait_send()
    scale(0)
    scale(1)

    far_x(0)
    give_out(0)
    own_y(3)
    fwd_y(2)
    far_x(1)
    give_out(1)
    send_x(6)
    fwd_x(4)
    fwd_y(3)
    far_y(2)
    far_x(2)
    give_out(2)
    far_y(3)
    scale(2)
    scale(3)

    @pl.loop(3, NC)
    def _(k):
        @pl.when(k + 4 < NC)
        def _():
            send_x(k + 4)

        @pl.when(k + 2 < NC)
        def _():
            fwd_x(k + 2)

        far_x(k)
        give_out(k)

        @pl.when(k < 6)
        def _():
            keep_out(k - 3)

        keep_out(k)

    @pl.loop(0, NC)
    def _(k):
        swap(k).wait_send()
        for copy in x_copies(k) + f_copies(k):
            copy.wait_send()
        o_copy(k).wait()
        c_copy(k).wait()


def on_device(hidden_act, out_grad, other_sq):
    dma = pltpu.SemaphoreType.DMA
    f32, bf16 = jnp.float32, jnp.bfloat16
    anywhere = pl.BlockSpec(memory_space=pl.ANY)
    return pl.pallas_call(
        kernel,
        out_shape=jax.ShapeDtypeStruct((D // 8, COLS), f32),
        in_specs=[anywhere, anywhere, anywhere, pl.BlockSpec(memory_space=pltpu.SMEM)],
        out_specs=anywhere,
        scratch_shapes=[
            pltpu.VMEM((TOK, COLS), bf16),
            pltpu.VMEM((NC, 4, 2, TOK, W), bf16),
            pltpu.VMEM((4, 4, 2, FEAT, TOK), bf16),
            pltpu.VMEM((TOK, FEAT), bf16),
            pltpu.VMEM((2, 2, L, L), f32),
            pltpu.VMEM((2, L, L), f32),
            pltpu.VMEM((2, L, L), f32),
            pltpu.VMEM((3, 2, ROWS, L), f32),
            pltpu.VMEM((2, ROWS, L), f32),
            pltpu.VMEM((2, ROWS, L), f32),
            pltpu.VMEM((4, 8, W), f32),
            pltpu.VMEM((3, 8, W), f32),
            pltpu.VMEM((8, W), f32),
            pltpu.VMEM((8, W), f32),
            pltpu.VMEM((3, 8, W), f32),
            pltpu.VMEM((8, 1, TOK), f32),
            pltpu.VMEM((NC, 2 * FEAT, W), f32),
            pltpu.VMEM((NC, 2 * FEAT, W), f32),
            dma((3,)), dma((NC,)), dma((2,)), dma((NC,)), dma((NC,)),
            dma((4, NC)), dma((4, NC)), dma((3,)), dma((3,)),
            dma((4, 4)), dma((4, 4)), dma((4, 4)), dma((4, 4)),
            dma((2,)), dma((3,)), dma((3,)), dma((2,)),
            dma((3,)), dma((3,)), dma((4,)), dma((3,)), dma((3,)),
            dma((NC,)), dma((NC,)), dma((NC,)),
        ],
        compiler_params=pltpu.CompilerParams(
            collective_id=0, has_side_effects=True, vmem_limit_bytes=60 * 2**20
        ),
    )(hidden_act, out_grad.T, out_grad, other_sq)


def solution(mesh):
    torus = Mesh(mesh.devices.reshape(4, 2, 4, 2, 2), AXES)
    dp, tensor = ("x", "zl"), ("y", "zh", "c")
    return jax.shard_map(
        on_device,
        mesh=torus,
        in_specs=(P(dp, tensor), P(dp, tensor), P(dp)),
        out_specs=P(dp, tensor),
        check_vma=False,
    )
```

time: 626 us -> 179 us (0.29)
  waiting for transfers between devices: 547 us -> 0 us
  Pallas kernels: 0 us -> 171 us
  matrix products: 32 us -> 0 us
  between operations: 13.2 us -> 0.01 us
  blocking collectives: 10.5 us -> 0 us
  starting transfers between devices: 8.13 us -> 0 us
    reduce_scatter x2 -> x0, waiting for transfers between devices: 480 us -> none  [summed_rows(): subtotal = lax.psum_scatter(subtotal, axis, scatter_dimension=0, tiled=True)]
    pallas_call x0 -> x1, Pallas kernels: none -> 171 us  [on_device(): pl.pallas_call(kernel, out_shape=jax.ShapeDtypeStruct((D // 8, COLS), f32...]
    all_gather x1 -> x0, waiting for transfers between devices: 43.1 us -> none  [on_device(): full_grad = lax.all_gather(out_grad, 'tensor', axis=1, tiled=True)]
    dot_general x3 -> x0, matrix products: 32 us -> none  [the longest x1 25.2 us: on_device(): lax.dot_general(scaled_grad, hidden_act, contract_rows, preferred_element...]
    all_to_all x1 -> x0, waiting for transfers between devices: 22.3 us -> none  [sum_at_owner(): lax.all_to_all(in_blocks(array, dim, length), axis, 0, 0, tiled=True)]
    all_to_all x1 -> x0, blocking collectives: 10.5 us -> none  [sent_to_all(): lax.all_to_all(jnp.broadcast_to(array[None], (length, *array.shape)), axi...]
    all_gather x1 -> x0, local copies, waits for them, and re-layouts: 9.44 us -> none  [on_device(): full_grad = lax.all_gather(out_grad, 'tensor', axis=1, tiled=True)]
    all_to_all x1 -> x0, starting transfers between devices: 8.04 us -> none  [sum_at_owner(): lax.all_to_all(in_blocks(array, dim, length), axis, 0, 0, tiled=True)]
  transfers between devices with their start and end apart: 4 -> 0, of which waited for: 4 -> 0; matrix products, arithmetic and copies ran while one was open for 1% -> 0% of each run, Pallas kernels for 0% -> 0%
where the time goes in v1:
time: 179 us
  Pallas kernels  171 us (96%)
  local copies, waits for them, and re-layouts  7.26 us (4%)
    pallas_call x1, Pallas kernels, on_device(): pl.pallas_call(kernel, out_shape=jax.ShapeDtypeStruct((D // 8, COLS), f32...  171 us
    unnamed x2, local copies, waits for them, and re-layouts  7.26 us

profile of v1, /device:TPU:0, one launch (start us, length us, event | category | flops | bytes accessed | tf_op | source)
XLA Modules:
  0.0 178.6 jit_solution(13994167886192970354)
XLA Ops:
  0.0 2.0 %copy.4.g_hbm = bf16[704,288]{1,0:T(8,128)(2,1)} copy(bf16[704,288]{0,1:T(8,128)(2,1)} %param.4) | data formatting | bytes 811008 | tf_op args[1]
  2.0 171.3 %shard_map.37 = f32[576,2304]{1,0:T(8,128)} custom-call(bf16[704,2304]{1,0:T(8,128)(2,1)} %hid_hbm.1, bf16[288,704]{1,0:T(8,128)(2,1)} %bitcast.1, bf16[704,288]{1,0:T(8,128)(2,1)} %copy.4.g_hbm, f32[2]{0:T(128)} %other_ref.1), custom_call_target="tpu_custom_call" | custom-call | tf_op jit(solution)/shard_map/pallas_call | solution.py:429
  173.3 5.2 %copy.6 = f32[576,2304]{1,0:T(8,128)} copy(f32[576,2304]{1,0:T(8,128)} %shard_map.37) | data formatting | bytes 10616832

commit v2 on v1

v2 whole, which is shorter than its diff:
```python
import functools
import math

import jax
import jax.numpy as jnp
from jax import lax
from jax.experimental import pallas as pl
from jax.experimental.pallas import tpu as pltpu
from jax.sharding import Mesh
from jax.sharding import PartitionSpec as P

D = 4608
FF = 36864
L = 352
TOK = 2 * L
COLS = 2304
HALF = COLS // 2
FEAT = 288
SUB = FEAT // 2
W = 128
NC = HALF // W
AXES = ("x", "zl", "y", "zh", "c")
MESH = pl.DeviceIdType.MESH
BOUND = math.sqrt(L * FF * D / 80.0)
NT = (((1,), (1,)), ((), ()))
PACK = 672
ROWS = PACK // 4


def kernel(
    hid_hbm, gt_hbm, g_hbm, other_ref, out_hbm,
    hid, bb, at, tb, gv, gh, rc, rd, ry, r2, rz, tl, ty, tc, tz, tx, sv, cs, co, cl,
    ld_s, lb_s, t_s, t_r, u_s, u_r, sw_s, sw_r, x_s, x_r, az_s, az_r, ay_s, ay_r, ac_s, ac_r,
    g1_s, g2_s, g2_r, g3_s, t1_s, t1_r, t2_s, t4_s, t4_r, c_s, c_r, o_s,
):
    x, zl, y, zh, c = (lax.axis_index(a) for a in AXES)
    z = zh * 2 + zl
    xr, xl, xo = (x + 1) % 4, (x + 3) % 4, (x + 2) % 4
    yr, yl, yo = (y + 1) % 4, (y + 3) % 4, (y + 2) % 4

    def dev(nx=None, nz=None, ny=None, nc=None):
        nz = z if nz is None else nz
        return (
            x if nx is None else nx,
            nz % 2,
            y if ny is None else ny,
            nz // 2,
            c if nc is None else nc,
        )

    zpair = zh * 2 + (1 - zl)

    def send(src, dst, ss, rs, to):
        return pltpu.make_async_remote_copy(
            src_ref=src, dst_ref=dst, send_sem=ss, recv_sem=rs,
            device_id=to, device_id_type=MESH,
        )

    keep = zl * HALF
    give = (1 - zl) * HALF

    load_hid = pltpu.make_async_copy(hid_hbm, hid, ld_s.at[0])
    load_g = pltpu.make_async_copy(g_hbm, gv, ld_s.at[1])
    load_hid.start()

    def load_own(k):
        col = pl.multiple_of(keep + k * W, W)
        return pltpu.make_async_copy(
            hid_hbm.at[:, pl.ds(col, W)], bb.at[k, x, zl], lb_s.at[k]
        )

    load_g.start()

    @pl.loop(0, NC)
    def _(k):
        load_own(k).start()

    def rows_of(j):
        return pl.ds(pl.multiple_of(j * SUB, 16), SUB)

    def t_copy(r):
        return send(
            gt_hbm.at[pl.ds(r * SUB, SUB)], tb.at[y % 2], t_s.at[r], t_r.at[y % 2],
            dev(ny=2 * c + r, nc=y // 2),
        )

    def t_here(r):
        return pltpu.make_async_copy(
            gt_hbm.at[pl.ds(r * SUB, SUB)], tb.at[y % 2], t_r.at[y % 2]
        )

    def u_copy(i):
        return send(
            tb.at[i], at.at[x, z, rows_of(y)], u_s.at[i], u_r.at[x % 2],
            dev(nx=2 * c + i, nc=x // 2),
        )

    bar = pltpu.get_barrier_semaphore()
    partners = [dev(nx=v) for v in (xr, xl, xo)]
    partners += [dev(ny=v) for v in (yr, yl, yo)]
    partners += [dev(nz=(z + d) % 4) for d in (1, 2, 3)]
    partners += [dev(nc=1 - c)]
    for to in partners:
        pl.semaphore_signal(bar, inc=1, device_id=to, device_id_type=MESH)

    count = len(partners)
    for i in range(2):
        for away, to in (
            (2 * c + i != y, dev(ny=2 * c + i, nc=y // 2)),
            (2 * c + i != x, dev(nx=2 * c + i, nc=x // 2)),
        ):
            count = count + away.astype(jnp.int32)

            @pl.when(away)
            def _():
                pl.semaphore_signal(bar, inc=1, device_id=to, device_id_type=MESH)

    pl.semaphore_wait(bar, count)

    for r in range(2):

        @pl.when(2 * c + r != y)
        def _():
            t_copy(r).start()

        @pl.when(2 * c + r == y)
        def _():
            t_here(r).start()

    def swap(k):
        col = pl.multiple_of(give + k * W, W)
        return send(
            hid.at[:, pl.ds(col, W)], bb.at[k, x, zl], sw_s.at[k], sw_r.at[k],
            dev(nz=zpair),
        )

    def x_copies(k):
        own, swapped = bb.at[k, x, zl], bb.at[k, x, 1 - zl]
        return (
            send(own, own, x_s.at[0, k], x_r.at[0, k], dev(nx=xr)),
            send(own, own, x_s.at[1, k], x_r.at[1, k], dev(nx=xl)),
            send(swapped, swapped, x_s.at[2, k], x_r.at[2, k], dev(nx=xr)),
            send(swapped, swapped, x_s.at[3, k], x_r.at[3, k], dev(nx=xl)),
        )

    def f_copies(k):
        a, b = bb.at[k, xl, 0], bb.at[k, xr, 1]
        return (
            send(a, a, x_s.at[4, k], x_r.at[4, k], dev(nx=xr)),
            send(b, b, x_s.at[5, k], x_r.at[5, k], dev(nx=xl)),
        )

    def own_x(k):
        load_own(k).wait()
        for copy in x_copies(k)[:2]:
            copy.start()

    def part_x(k):
        swap(k).wait_recv()
        for copy in x_copies(k)[2:]:
            copy.start()

    def fwd_x(k):
        for copy in x_copies(k):
            copy.wait_recv()
        for copy in f_copies(k):
            copy.start()

    def far_x(k):
        for copy in f_copies(k):
            copy.wait_recv()

    load_hid.wait()
    swap(0).start()
    swap(1).start()
    own_x(0)

    def pack(e, kind, gram):
        gh[e, kind, 0:352, :] = gram[:, 0:128]
        gh[e, kind, 352:576, :] = gram[128:352, 128:256]
        gh[e, kind, 576:672, :] = jnp.zeros((96, W), jnp.float32)
        gh[e, kind, 576:672, 0:96] = gram[256:352, 256:352]

    @pl.loop(0, 2)
    def _(e):
        rows = pl.ds(pl.multiple_of(e * L, 32), L)
        h = hid[rows, :]
        pack(e, 0, lax.dot_general(h, h, NT, preferred_element_type=jnp.float32))

    load_g.wait()

    @pl.loop(0, 2)
    def _(e):
        rows = pl.ds(pl.multiple_of(e * L, 32), L)
        g = gv[rows, :]
        pack(e, 1, lax.dot_general(g, g, NT, preferred_element_type=jnp.float32))

    g1 = send(gh.at[1 - c], rc, g1_s.at[0], g1_s.at[1], dev(nc=1 - c))
    g1.start()

    zr, zb = (z + 1) % 4, (z + 3) % 4

    def piece(i, zz, yy):
        return at.at[2 * c + i, zz, rows_of(yy)]

    def z_copies(i):
        b = piece(i, z, y)
        return (
            send(b, b, az_s.at[i], az_r.at[i], dev(nz=zr)),
            send(b, b, az_s.at[2 + i], az_r.at[2 + i], dev(nz=zb)),
        )

    def zf_copies():
        a, b = piece(0, zb, y), piece(1, zr, y)
        return (
            send(a, a, az_s.at[4], az_r.at[4], dev(nz=zr)),
            send(b, b, az_s.at[5], az_r.at[5], dev(nz=zb)),
        )

    middle = zl != zh
    inner = z // 2 * 2 + (1 - zl)
    outer = (z + 2 * zl + 3) % 4
    across = (z + 2) % 4

    def block(q):
        there = (z, inner, outer, across)[q]
        return jnp.where(middle, there, (outer, across, z, inner)[q])

    def y_copies(q, i):
        b = piece(i, block(q), y)
        return (
            send(b, b, ay_s.at[i, q], ay_r.at[i, q], dev(ny=yr)),
            send(b, b, ay_s.at[2 + i, q], ay_r.at[2 + i, q], dev(ny=yl)),
        )

    def yf_copies(q):
        a, b = piece(0, block(q), yl), piece(1, block(q), yr)
        return (
            send(a, a, ay_s.at[4, q], ay_r.at[4, q], dev(ny=yr)),
            send(b, b, ay_s.at[5, q], ay_r.at[5, q], dev(ny=yl)),
        )

    def core_copy(q, j):
        b = at.at[pl.ds(2 * c, 2), block(q), rows_of((y, yl, yr, yo)[j])]
        return send(b, b, ac_s.at[j, q], ac_r.at[j, q], dev(nc=1 - c))

    def own_y(q):
        for i in range(2):
            for copy in y_copies(q, i):
                copy.start()
        core_copy(q, 0).start()

    def fwd_y(q):
        y_copies(q, 0)[0].wait_recv()
        yf_copies(q)[0].start()
        y_copies(q, 1)[1].wait_recv()
        yf_copies(q)[1].start()
        y_copies(q, 1)[0].wait_recv()
        core_copy(q, 1).start()
        y_copies(q, 0)[1].wait_recv()
        core_copy(q, 2).start()

    def far_y(q):
        for copy in yf_copies(q):
            copy.wait_recv()
        core_copy(q, 3).start()

    def settle(q):
        for copy in y_copies(q, 0) + y_copies(q, 1) + yf_copies(q):
            copy.wait_send()
        for j in range(4):
            core_copy(q, j).wait()

    def scale(q):
        settle(q)

        @pl.loop(0, 8)
        def _(i):
            xs = i // 2
            rows = pl.ds(pl.multiple_of(i % 2 * FEAT, 32), FEAT)
            s = sv[xs * 2 + block(q) % 2]
            b = at[xs, block(q), rows].astype(jnp.float32)
            at[xs, block(q), rows] = (b * s).astype(jnp.bfloat16)

    def g2(d):
        to = (y + d) % 4
        rows = pl.ds(pl.multiple_of(to * ROWS, 8), ROWS)
        return send(
            rd.at[:, rows, :], ry.at[d - 1], g2_s.at[d - 1], g2_r.at[d - 1], dev(ny=to)
        )

    part_x(0)
    swap(2).start()
    swap(3).start()
    for i in range(2):
        pltpu.make_async_copy(gt_hbm.at[pl.ds(0, SUB)], tb.at[i], t_r.at[i]).wait()

    for i in range(2):
        far_plane = 2 * c + i != x

        @pl.when(far_plane)
        def _():
            u_copy(i).start()

        @pl.when(jnp.logical_not(far_plane))
        def _():
            at[x, z, rows_of(y)] = tb[i]

    own_x(1)
    g1.wait()
    rd[...] = gh[c] + rc[...]
    for d in (2, 1, 3):
        g2(d).start()
    part_x(1)
    own_x(2)

    for i in range(2):

        @pl.when(2 * c + i != x)
        def _():
            send(
                tb.at[i], at.at[2 * c + i, z, rows_of(y)], u_s.at[i], u_r.at[i],
                dev(nx=2 * c + i, nc=x // 2),
            ).wait_recv()

        for copy in z_copies(i):
            copy.start()

        @pl.when(middle)
        def _():
            for copy in y_copies(0, i):
                copy.start()

    @pl.when(middle)
    def _():
        core_copy(0, 0).start()

    own_x(3)
    fwd_x(0)
    part_x(2)

    for d in (2, 1, 3):
        g2(d).wait()
    mine = pl.ds(pl.multiple_of(y * ROWS, 8), ROWS)
    r2[...] = rd[:, mine, :] + ry[0] + ry[1] + ry[2]
    g3 = send(r2, rz, g3_s.at[0], g3_s.at[1], dev(nz=across))
    g3.start()

    z_copies(0)[0].wait_recv()
    zf_copies()[0].start()
    z_copies(0)[1].wait_recv()
    z_copies(1)[1].wait_recv()
    zf_copies()[1].start()
    z_copies(1)[0].wait_recv()
    swap(4).start()

    @pl.when(jnp.logical_not(middle))
    def _():
        own_y(0)

    part_x(3)
    fwd_x(1)
    own_x(4)
    g3.wait()
    total = r2[...] + rz[...]
    at_row = lax.broadcasted_iota(jnp.int32, (ROWS, W), 0) + y * ROWS
    at_lane = lax.broadcasted_iota(jnp.int32, (ROWS, W), 1)
    tile_of = (at_row >= 352).astype(jnp.int32) + (at_row >= 576).astype(jnp.int32)
    over = at_row - jnp.where(tile_of == 0, 0, jnp.where(tile_of == 1, 352, 576)) - at_lane
    weight = jnp.where(over > 0, 2.0, jnp.where(over == 0, 1.0, 0.0))
    part = jnp.sum(total[0] * total[1] * weight)
    lane = lax.broadcasted_iota(jnp.int32, (8, W), 1)
    example = (x * 2 + zl) * 2 + c
    other = jnp.where(c == 0, other_ref[0], other_ref[1])
    tile = jnp.where(lane == example * 4 + y, part, 0.0)
    tl[0] = tile + jnp.where((lane == 64 + example) & (y == 0), other, 0.0)

    def t1(d):
        return send(
            tl.at[0], ty.at[d - 1], t1_s.at[d - 1], t1_r.at[d - 1], dev(ny=(y + d) % 4)
        )

    for d in (2, 1, 3):
        t1(d).start()

    @pl.when(middle)
    def _():
        own_y(1)

    for copy in zf_copies():
        copy.wait_recv()

    @pl.when(jnp.logical_not(middle))
    def _():
        own_y(1)

    swap(5).start()
    fwd_y(0)

    for d in (2, 1, 3):
        t1(d).wait()
    tl[1] = tl[0] + ty[0] + ty[1] + ty[2]
    t2 = send(tl.at[1], tc, t2_s.at[0], t2_s.at[1], dev(nc=1 - c))
    t2.start()
    t2.wait()
    tl[2] = tl[1] + tc[...]
    t3 = send(tl.at[2], tz, t2_s.at[2], t2_s.at[3], dev(nz=zpair))
    t3.start()
    t3.wait()
    tl[3] = tl[2] + tz[...]

    def t4(d):
        return send(
            tl.at[3], tx.at[d - 1], t4_s.at[d - 1], t4_r.at[d - 1], dev(nx=(x + d) % 4)
        )

    for d in (2, 1, 3):
        t4(d).start()

    fwd_x(2)
    part_x(4)
    own_x(5)
    swap(6).start()
    fwd_y(1)
    own_y(2)
    part_x(5)
    swap(7).start()
    swap(8).start()
    far_y(0)
    own_x(6)
    own_y(3)

    for d in (2, 1, 3):
        t4(d).wait()
    full = (tl[3] + tx[0] + tx[1] + tx[2])[0:1]
    row = lax.broadcasted_iota(jnp.int32, (1, W), 1)
    token = lax.broadcasted_iota(jnp.int32, (1, TOK), 1)
    for g in range(8):
        pair = []
        for e in (2 * g, 2 * g + 1):
            layer = jnp.sum(
                jnp.where((row >= 4 * e) & (row < 4 * e + 4), full, 0.0), axis=1, keepdims=True
            )
            rest = jnp.sum(jnp.where(row == 64 + e, full, 0.0), axis=1, keepdims=True)
            pair.append(jnp.minimum(1.0, BOUND / jnp.sqrt(rest + layer)))
        sv[g] = jnp.where(token < L, pair[0], pair[1])

    for i in range(2):

        @pl.when(2 * c + i != y)
        def _():
            t_copy(i).wait_send()

        @pl.when(2 * c + i != x)
        def _():
            u_copy(i).wait_send()

    for copy in z_copies(0) + z_copies(1) + zf_copies():
        copy.wait_send()
    far_y(1)
    fwd_x(3)
    scale(0)
    scale(1)

    def multiply(high, rhs, put):
        @pl.loop(0, 2)
        def _(cc):
            rows = pl.ds(pl.multiple_of(cc * FEAT, 32), FEAT)
            acc = None
            for xs in range(4):
                for zs in range(2):
                    p = jnp.dot(
                        at[xs, high * 2 + zs, rows], rhs(xs, zs),
                        preferred_element_type=jnp.float32,
                    )
                    acc = p if acc is None else acc + p
            put(rows, acc)

    def out_cols(k, width):
        return out_hbm.at[:, pl.ds(pl.multiple_of(keep + k * W, W), width)]

    def c_copy(k):
        return send(cs.at[k], out_cols(k, W), c_s.at[k], c_r.at[k], dev(nz=zpair))

    def o_copy(i):
        return pltpu.make_async_copy(co.at[i], out_cols(2 * i, 2 * W), o_s.at[i])

    def give_out(k):
        def put(rows, acc):
            cs[k, rows, :] = acc

        multiply(1 - zl, lambda xs, zs: bb[k, xs, zs], put)
        c_copy(k).start()

    def keep_out(i):
        def put(rows, acc):
            co[i, rows, :] = acc

        def rhs(xs, zs):
            return jnp.concatenate([bb[2 * i, xs, zs], bb[2 * i + 1, xs, zs]], axis=1)

        multiply(zl, rhs, put)
        o_copy(i).start()

    last_copy = pltpu.make_async_copy(cl, out_cols(NC - 1, W), o_s.at[4])

    def keep_last():
        def put(rows, acc):
            cl[rows, :] = acc

        multiply(zl, lambda xs, zs: bb[NC - 1, xs, zs], put)
        last_copy.start()

    def serve_x(k):
        @pl.when(k + 5 < NC)
        def _():
            own_x(k + 5)

        @pl.when(k + 4 < NC)
        def _():
            part_x(k + 4)

        @pl.when(k + 2 < NC)
        def _():
            fwd_x(k + 2)

    @pl.loop(0, 5)
    def _(k):
        @pl.when(k >= 2)
        def _():
            serve_x(k)

        far_x(k)
        give_out(k)

        @pl.when(k == 2)
        def _():
            fwd_y(2)

        @pl.when(k == 3)
        def _():
            far_y(2)

    fwd_y(3)
    far_y(3)
    scale(2)
    scale(3)

    @pl.loop(5, NC)
    def _(k):
        serve_x(k)
        far_x(k)
        give_out(k)

        @pl.loop(jnp.where(k == 5, 0, k - 4), jnp.minimum(k - 3, 4))
        def _(i):
            keep_out(i)

    keep_last()

    @pl.loop(0, NC)
    def _(k):
        swap(k).wait_send()
        for copy in x_copies(k) + f_copies(k):
            copy.wait_send()
        c_copy(k).wait()

    @pl.loop(0, 4)
    def _(i):
        o_copy(i).wait()

    last_copy.wait()


def on_device(hidden_act, out_grad, other_sq):
    dma = pltpu.SemaphoreType.DMA
    f32, bf16 = jnp.float32, jnp.bfloat16
    anywhere = pl.BlockSpec(memory_space=pl.ANY)
    return pl.pallas_call(
        kernel,
        out_shape=jax.ShapeDtypeStruct((D // 8, COLS), f32),
        in_specs=[anywhere, anywhere, anywhere, pl.BlockSpec(memory_space=pltpu.SMEM)],
        out_specs=anywhere,
        scratch_shapes=[
            pltpu.VMEM((TOK, COLS), bf16),
            pltpu.VMEM((NC, 4, 2, TOK, W), bf16),
            pltpu.VMEM((4, 4, 2 * FEAT, TOK), bf16),
            pltpu.VMEM((2, SUB, TOK), bf16),
            pltpu.VMEM((TOK, FEAT), bf16),
            pltpu.VMEM((2, 2, PACK, W), f32),
            pltpu.VMEM((2, PACK, W), f32),
            pltpu.VMEM((2, PACK, W), f32),
            pltpu.VMEM((3, 2, ROWS, W), f32),
            pltpu.VMEM((2, ROWS, W), f32),
            pltpu.VMEM((2, ROWS, W), f32),
            pltpu.VMEM((4, 8, W), f32),
            pltpu.VMEM((3, 8, W), f32),
            pltpu.VMEM((8, W), f32),
            pltpu.VMEM((8, W), f32),
            pltpu.VMEM((3, 8, W), f32),
            pltpu.VMEM((8, 1, TOK), f32),
            pltpu.VMEM((NC, 2 * FEAT, W), f32),
            pltpu.VMEM((4, 2 * FEAT, 2 * W), f32),
            pltpu.VMEM((2 * FEAT, W), f32),
            dma((2,)), dma((NC,)), dma((2,)), dma((2,)), dma((2,)), dma((2,)), dma((NC,)), dma((NC,)),
            dma((6, NC)), dma((6, NC)), dma((6,)), dma((6,)),
            dma((6, 4)), dma((6, 4)), dma((4, 4)), dma((4, 4)),
            dma((2,)), dma((3,)), dma((3,)), dma((2,)),
            dma((3,)), dma((3,)), dma((4,)), dma((3,)), dma((3,)),
            dma((NC,)), dma((NC,)), dma((5,)),
        ],
        compiler_params=pltpu.CompilerParams(
            collective_id=0, has_side_effects=True, vmem_limit_bytes=60 * 2**20
        ),
    )(hidden_act, out_grad.T, out_grad, other_sq)


def solution(mesh):
    torus = Mesh(mesh.devices.reshape(4, 2, 4, 2, 2), AXES)
    dp, tensor = ("x", "zl"), ("y", "zh", "c")
    return jax.shard_map(
        on_device,
        mesh=torus,
        in_specs=(P(dp, tensor), P(dp, tensor), P(dp)),
        out_specs=P(dp, tensor),
        check_vma=False,
    )
```

time: 179 us -> 146 us (0.82)
  Pallas kernels: 171 us -> 137 us
    pallas_call x1, Pallas kernels: 171 us -> 137 us  [on_device(): pl.pallas_call(kernel, out_shape=jax.ShapeDtypeStruct((D // 8, COLS), f32...]
where the time goes in v2:
time: 146 us; the launch traced here: 144 us
  Pallas kernels  137 us (94%)
  local copies, waits for them, and re-layouts  7.26 us (5%)
    pallas_call x1, Pallas kernels, on_device(): pl.pallas_call(kernel, out_shape=jax.ShapeDtypeStruct((D // 8, COLS), f32...  137 us
    unnamed x2, local copies, waits for them, and re-layouts  7.26 us

profile of v2, /device:TPU:0, one launch (start us, length us, event | category | flops | bytes accessed | tf_op | source)
XLA Modules:
  0.0 143.8 jit_solution(6108901087708751741)
XLA Ops:
  0.0 2.0 %copy.4.g_hbm = bf16[704,288]{1,0:T(8,128)(2,1)} copy(bf16[704,288]{0,1:T(8,128)(2,1)} %param.4) | data formatting | bytes 811008 | tf_op args[1]
  2.0 136.5 %shard_map.37 = f32[576,2304]{1,0:T(8,128)} custom-call(bf16[704,2304]{1,0:T(8,128)(2,1)} %hid_hbm.1, bf16[288,704]{1,0:T(8,128)(2,1)} %bitcast.1, bf16[704,288]{1,0:T(8,128)(2,1)} %copy.4.g_hbm, f32[2]{0:T(128)} %other_ref.1), custom_call_target="tpu_custom_call" | custom-call | tf_op jit(solution)/shard_map/pallas_call | solution.py:579
  138.6 5.2 %copy.6 = f32[576,2304]{1,0:T(8,128)} copy(f32[576,2304]{1,0:T(8,128)} %shard_map.37) | data formatting | bytes 10616832

commit v3 on v2

--- a/solution.py
+++ b/solution.py
@@ -18,6 +18,7 @@
 FEAT = 288
 SUB = FEAT // 2
 W = 128
+VMEM_LIMIT = 61_400_000
 NC = HALF // W
 AXES = ("x", "zl", "y", "zh", "c")
 MESH = pl.DeviceIdType.MESH
@@ -28,10 +29,10 @@
 
 
 def kernel(
-    hid_hbm, gt_hbm, g_hbm, other_ref, out_hbm,
-    hid, bb, at, tb, gv, gh, rc, rd, ry, r2, rz, tl, ty, tc, tz, tx, sv, cs, co, cl,
+    hid_hbm, gt_hbm, other_ref, out,
+    hid, bb, at, tb, gv, gh, rc, rd, ry, r2, rz, tl, ty, tc, tz, tx, sv, cs,
     ld_s, lb_s, t_s, t_r, u_s, u_r, sw_s, sw_r, x_s, x_r, az_s, az_r, ay_s, ay_r, ac_s, ac_r,
-    g1_s, g2_s, g2_r, g3_s, t1_s, t1_r, t2_s, t4_s, t4_r, c_s, c_r, o_s,
+    g1_s, g2_s, g2_r, g3_s, t1_s, t1_r, t2_s, t4_s, t4_r, c_s, c_r,
 ):
     x, zl, y, zh, c = (lax.axis_index(a) for a in AXES)
     z = zh * 2 + zl
@@ -60,7 +61,7 @@
     give = (1 - zl) * HALF
 
     load_hid = pltpu.make_async_copy(hid_hbm, hid, ld_s.at[0])
-    load_g = pltpu.make_async_copy(g_hbm, gv, ld_s.at[1])
+    load_g = pltpu.make_async_copy(gt_hbm, gv, ld_s.at[1])
     load_hid.start()
 
     def load_own(k):
@@ -174,6 +175,7 @@
     swap(0).start()
     swap(1).start()
     own_x(0)
+    own_x(1)
 
     def pack(e, kind, gram):
         gh[e, kind, 0:352, :] = gram[:, 0:128]
@@ -188,11 +190,9 @@
         pack(e, 0, lax.dot_general(h, h, NT, preferred_element_type=jnp.float32))
 
     load_g.wait()
-
-    @pl.loop(0, 2)
-    def _(e):
-        rows = pl.ds(pl.multiple_of(e * L, 32), L)
-        g = gv[rows, :]
+    turned = jnp.transpose(gv[...])
+    for e in range(2):
+        g = turned[e * L : (e + 1) * L]
         pack(e, 1, lax.dot_general(g, g, NT, preferred_element_type=jnp.float32))
 
     g1 = send(gh.at[1 - c], rc, g1_s.at[0], g1_s.at[1], dev(nc=1 - c))
@@ -289,7 +289,6 @@
             rd.at[:, rows, :], ry.at[d - 1], g2_s.at[d - 1], g2_r.at[d - 1], dev(ny=to)
         )
 
-    part_x(0)
     swap(2).start()
     swap(3).start()
     for i in range(2):
@@ -306,7 +305,7 @@
         def _():
             at[x, z, rows_of(y)] = tb[i]
 
-    own_x(1)
+    part_x(0)
     g1.wait()
     rd[...] = gh[c] + rc[...]
     for d in (2, 1, 3):
@@ -336,7 +335,6 @@
         core_copy(0, 0).start()
 
     own_x(3)
-    fwd_x(0)
     part_x(2)
 
     for d in (2, 1, 3):
@@ -358,9 +356,14 @@
     def _():
         own_y(0)
 
+    @pl.when(middle)
+    def _():
+        own_y(1)
+
+    fwd_x(0)
     part_x(3)
+    own_x(4)
     fwd_x(1)
-    own_x(4)
     g3.wait()
     total = r2[...] + rz[...]
     at_row = lax.broadcasted_iota(jnp.int32, (ROWS, W), 0) + y * ROWS
@@ -383,10 +386,6 @@
     for d in (2, 1, 3):
         t1(d).start()
 
-    @pl.when(middle)
-    def _():
-        own_y(1)
-
     for copy in zf_copies():
         copy.wait_recv()
 
@@ -424,10 +423,10 @@
     fwd_y(1)
     own_y(2)
     part_x(5)
+    own_x(6)
     swap(7).start()
     swap(8).start()
     far_y(0)
-    own_x(6)
     own_y(3)
 
     for d in (2, 1, 3):
@@ -474,42 +473,37 @@
                         preferred_element_type=jnp.float32,
                     )
                     acc = p if acc is None else acc + p
-            put(rows, acc)
-
-    def out_cols(k, width):
-        return out_hbm.at[:, pl.ds(pl.multiple_of(keep + k * W, W), width)]
-
-    def c_copy(k):
-        return send(cs.at[k], out_cols(k, W), c_s.at[k], c_r.at[k], dev(nz=zpair))
-
-    def o_copy(i):
-        return pltpu.make_async_copy(co.at[i], out_cols(2 * i, 2 * W), o_s.at[i])
+            put(cc, rows, acc)
+
+    def c_copy(k, cc):
+        rows = pl.ds(pl.multiple_of(cc * FEAT, 32), FEAT)
+        cols = pl.ds(pl.multiple_of(keep + k * W, W), W)
+        return send(
+            cs.at[k, rows], out.at[rows, cols], c_s.at[cc, k], c_r.at[cc, k],
+            dev(nz=zpair),
+        )
 
     def give_out(k):
-        def put(rows, acc):
+        def put(cc, rows, acc):
             cs[k, rows, :] = acc
+            c_copy(k, cc).start()
 
         multiply(1 - zl, lambda xs, zs: bb[k, xs, zs], put)
-        c_copy(k).start()
 
     def keep_out(i):
-        def put(rows, acc):
-            co[i, rows, :] = acc
+        def put(cc, rows, acc):
+            out[rows, pl.ds(pl.multiple_of(keep + i * 2 * W, W), 2 * W)] = acc
 
         def rhs(xs, zs):
             return jnp.concatenate([bb[2 * i, xs, zs], bb[2 * i + 1, xs, zs]], axis=1)
 
         multiply(zl, rhs, put)
-        o_copy(i).start()
-
-    last_copy = pltpu.make_async_copy(cl, out_cols(NC - 1, W), o_s.at[4])
 
     def keep_last():
-        def put(rows, acc):
-            cl[rows, :] = acc
+        def put(cc, rows, acc):
+            out[rows, pl.ds(pl.multiple_of(keep + (NC - 1) * W, W), W)] = acc
 
         multiply(zl, lambda xs, zs: bb[NC - 1, xs, zs], put)
-        last_copy.start()
 
     def serve_x(k):
         @pl.when(k + 5 < NC)
@@ -526,35 +520,36 @@
 
     @pl.loop(0, 5)
     def _(k):
-        @pl.when(k >= 2)
-        def _():
-            serve_x(k)
-
         far_x(k)
         give_out(k)
 
-        @pl.when(k == 2)
+        @pl.when(k == 1)
         def _():
             fwd_y(2)
 
+        @pl.when(k >= 2)
+        def _():
+            serve_x(k)
+
         @pl.when(k == 3)
         def _():
-            far_y(2)
-
-    fwd_y(3)
+            fwd_y(3)
+
+    far_y(2)
     far_y(3)
     scale(2)
     scale(3)
 
     @pl.loop(5, NC)
     def _(k):
-        serve_x(k)
         far_x(k)
         give_out(k)
 
         @pl.loop(jnp.where(k == 5, 0, k - 4), jnp.minimum(k - 3, 4))
         def _(i):
             keep_out(i)
+
+        serve_x(k)
 
     keep_last()
 
@@ -563,30 +558,25 @@
         swap(k).wait_send()
         for copy in x_copies(k) + f_copies(k):
             copy.wait_send()
-        c_copy(k).wait()
-
-    @pl.loop(0, 4)
-    def _(i):
-        o_copy(i).wait()
-
-    last_copy.wait()
+        for cc in range(2):
+            c_copy(k, cc).wait()
 
 
 def on_device(hidden_act, out_grad, other_sq):
     dma = pltpu.SemaphoreType.DMA
     f32, bf16 = jnp.float32, jnp.bfloat16
-    anywhere = pl.BlockSpec(memory_space=pl.ANY)
+    anywhere = pl.BlockSpec(memory_space=pltpu.HBM)
     return pl.pallas_call(
         kernel,
-        out_shape=jax.ShapeDtypeStruct((D // 8, COLS), f32),
-        in_specs=[anywhere, anywhere, anywhere, pl.BlockSpec(memory_space=pltpu.SMEM)],
-        out_specs=anywhere,
+        out_shape=pltpu.VMEM((D // 8, COLS), f32),
+        in_specs=[anywhere, anywhere, pl.BlockSpec(memory_space=pltpu.SMEM)],
+        out_specs=pl.BlockSpec(memory_space=pltpu.VMEM),
         scratch_shapes=[
             pltpu.VMEM((TOK, COLS), bf16),
             pltpu.VMEM((NC, 4, 2, TOK, W), bf16),
             pltpu.VMEM((4, 4, 2 * FEAT, TOK), bf16),
             pltpu.VMEM((2, SUB, TOK), bf16),
-            pltpu.VMEM((TOK, FEAT), bf16),
+            pltpu.VMEM((FEAT, TOK), bf16),
             pltpu.VMEM((2, 2, PACK, W), f32),
             pltpu.VMEM((2, PACK, W), f32),
             pltpu.VMEM((2, PACK, W), f32),
@@ -600,19 +590,17 @@
             pltpu.VMEM((3, 8, W), f32),
             pltpu.VMEM((8, 1, TOK), f32),
             pltpu.VMEM((NC, 2 * FEAT, W), f32),
-            pltpu.VMEM((4, 2 * FEAT, 2 * W), f32),
-            pltpu.VMEM((2 * FEAT, W), f32),
             dma((2,)), dma((NC,)), dma((2,)), dma((2,)), dma((2,)), dma((2,)), dma((NC,)), dma((NC,)),
             dma((6, NC)), dma((6, NC)), dma((6,)), dma((6,)),
             dma((6, 4)), dma((6, 4)), dma((4, 4)), dma((4, 4)),
             dma((2,)), dma((3,)), dma((3,)), dma((2,)),
             dma((3,)), dma((3,)), dma((4,)), dma((3,)), dma((3,)),
-            dma((NC,)), dma((NC,)), dma((5,)),
+            dma((2, NC)), dma((2, NC)),
         ],
         compiler_params=pltpu.CompilerParams(
-            collective_id=0, has_side_effects=True, vmem_limit_bytes=60 * 2**20
+            collective_id=0, has_side_effects=True, vmem_limit_bytes=VMEM_LIMIT
         ),
-    )(hidden_act, out_grad.T, out_grad, other_sq)
+    )(hidden_act, out_grad.T, other_sq)
 
 
 def solution(mesh):

time: 146 us -> 139 us (0.952); the launches traced: 144 us -> 139 us
  local copies, waits for them, and re-layouts: 7.26 us -> 2.38 us
    unnamed x2 -> x1, local copies, waits for them, and re-layouts: 7.26 us -> 2.38 us
where the time goes in v3:
time: 139 us
  Pallas kernels  136 us (98%)
  local copies, waits for them, and re-layouts  2.38 us (2%)
    pallas_call x1, Pallas kernels, on_device(): pl.pallas_call(kernel, out_shape=pltpu.VMEM((D // 8, COLS), f32), in_spec...  136 us

profile of v3, /device:TPU:0, one launch (start us, length us, event | category | flops | bytes accessed | tf_op | source)
XLA Modules:
  0.0 138.7 jit_solution(3633418719062175917)
XLA Ops:
  0.0 136.3 %shard_map.37 = f32[576,2304]{1,0:T(8,128)S(1)} custom-call(bf16[704,2304]{1,0:T(8,128)(2,1)} %hid_hbm.1, bf16[288,704]{1,0:T(8,128)(2,1)} %bitcast.1, f32[2]{0:T(128)} %other_ref.1), custom_call_target="tpu_custom_call" | custom-call | tf_op jit(solution)/shard_map/pallas_call | solution.py:569
  136.3 2.4 %copy.5 = f32[576,2304]{1,0:T(8,128)} copy(f32[576,2304]{1,0:T(8,128)S(1)} %shard_map.37) | data formatting | bytes 10616832

commit v4 on v3

--- a/solution.py
+++ b/solution.py
@@ -506,6 +506,10 @@
         multiply(zl, lambda xs, zs: bb[NC - 1, xs, zs], put)
 
     def serve_x(k):
+        @pl.when(k + 2 < NC)
+        def _():
+            fwd_x(k + 2)
+
         @pl.when(k + 5 < NC)
         def _():
             own_x(k + 5)
@@ -513,10 +517,6 @@
         @pl.when(k + 4 < NC)
         def _():
             part_x(k + 4)
-
-        @pl.when(k + 2 < NC)
-        def _():
-            fwd_x(k + 2)
 
     @pl.loop(0, 5)
     def _(k):

time: 139 us -> 138 us (level); the launches traced: 139 us -> 136 us
  Pallas kernels: 136 us -> 134 us
    pallas_call x1, Pallas kernels: 136 us -> 134 us  [on_device(): pl.pallas_call(kernel, out_shape=pltpu.VMEM((D // 8, COLS), f32), in_spec...]
where the time goes in v4:
time: 138 us; the launch traced here: 136 us
  Pallas kernels  134 us (97%)
  local copies, waits for them, and re-layouts  2.38 us (2%)
    pallas_call x1, Pallas kernels, on_device(): pl.pallas_call(kernel, out_shape=pltpu.VMEM((D // 8, COLS), f32), in_spec...  134 us

profile of v4, /device:TPU:0, one launch (start us, length us, event | category | flops | bytes accessed | tf_op | source)
XLA Modules:
  0.0 136.2 jit_solution(15342361714084241559)
XLA Ops:
  0.0 133.8 %shard_map.37 = f32[576,2304]{1,0:T(8,128)S(1)} custom-call(bf16[704,2304]{1,0:T(8,128)(2,1)} %hid_hbm.1, bf16[288,704]{1,0:T(8,128)(2,1)} %bitcast.1, f32[2]{0:T(128)} %other_ref.1), custom_call_target="tpu_custom_call" | custom-call | tf_op jit(solution)/shard_map/pallas_call | solution.py:569
  133.8 2.4 %copy.5 = f32[576,2304]{1,0:T(8,128)} copy(f32[576,2304]{1,0:T(8,128)S(1)} %shard_map.37) | data formatting | bytes 10616832

commit v5 on v4

--- a/solution.py
+++ b/solution.py
@@ -506,17 +506,30 @@
         multiply(zl, lambda xs, zs: bb[NC - 1, xs, zs], put)
 
     def serve_x(k):
-        @pl.when(k + 2 < NC)
+        @pl.when(k < 6)
         def _():
             fwd_x(k + 2)
 
-        @pl.when(k + 5 < NC)
-        def _():
-            own_x(k + 5)
-
-        @pl.when(k + 4 < NC)
-        def _():
-            part_x(k + 4)
+        @pl.when(k == 2)
+        def _():
+            own_x(7)
+            part_x(6)
+
+        @pl.when(k == 3)
+        def _():
+            part_x(7)
+
+        @pl.when(k == 4)
+        def _():
+            own_x(8)
+
+        @pl.when(k == 5)
+        def _():
+            part_x(8)
+
+        @pl.when(k == 7)
+        def _():
+            fwd_x(8)
 
     @pl.loop(0, 5)
     def _(k):

time: 138 us -> 137 us (level)
  Pallas kernels: 134 us -> 132 us
    pallas_call x1, Pallas kernels: 134 us -> 132 us  [on_device(): pl.pallas_call(kernel, out_shape=pltpu.VMEM((D // 8, COLS), f32), in_spec...]
where the time goes in v5:
time: 137 us; the launch traced here: 134 us
  Pallas kernels  132 us (96%)
  local copies, waits for them, and re-layouts  2.38 us (2%)
    pallas_call x1, Pallas kernels, on_device(): pl.pallas_call(kernel, out_shape=pltpu.VMEM((D // 8, COLS), f32), in_spec...  132 us

profile of v5, /device:TPU:0, one launch (start us, length us, event | category | flops | bytes accessed | tf_op | source)
XLA Modules:
  0.0 134.2 jit_solution(17469538355494974227)
XLA Ops:
  0.0 131.8 %shard_map.37 = f32[576,2304]{1,0:T(8,128)S(1)} custom-call(bf16[704,2304]{1,0:T(8,128)(2,1)} %hid_hbm.1, bf16[288,704]{1,0:T(8,128)(2,1)} %bitcast.1, f32[2]{0:T(128)} %other_ref.1), custom_call_target="tpu_custom_call" | custom-call | tf_op jit(solution)/shard_map/pallas_call | solution.py:582
  131.8 2.4 %copy.5 = f32[576,2304]{1,0:T(8,128)} copy(f32[576,2304]{1,0:T(8,128)S(1)} %shard_map.37) | data formatting | bytes 10616832
